TPU v7x, 32 devices: a whole 2x2x4 slice. The times are simulated.
32 devices in a mesh: dp: 4 (over y, core), slab: 8 (over z, x).
Axes of the slice: x: 2, y: 2, z: 4, core: 2. Of those that a mesh axis runs over, the one named last changes fastest.
Arguments:
- acts: bfloat16 [4, 32, 8, 128, 128], P('dp', None, 'slab'), may hold values from -24 to 24
- grads: bfloat16 [4, 32, 8, 128, 128], P('dp', None, 'slab'), may hold values from -6 to 6
- picks: int32 [4, 4096], P('dp', 'slab'), may hold values from 0 to 31
Outputs:
- weight_grad: float32 [32, 864], replicated
- update: float32 [32, 864], replicated
Inputs may be any that keep to these rules, and one draw needn't show every extreme that they name: `picks`: one cell is sampled in each aligned block of 32 of a device's cells, counted plane by plane, row by row, column by column; entry e of a device's 512 entries belongs to block e.
All inputs are finite; a program needn't handle non-finite values.
Results may differ from a plain program's by a relative error of at most 0.0003.
Values may be sent and summed in bfloat16 or wider, within the bound.
A program may use at most 128 MiB of HBM per device.

v0:
```python
import math
import jax
import jax.numpy as jnp
from jax import lax
from jax.sharding import PartitionSpec as P

epsilon = 1e-06
damping = 0.1
trust_region_limit = 0.3
learning_rate = 0.01


def padded_2(shard, sides, width):
    for axis, dim in sides:
        size, length = (lax.axis_size(axis), shard.shape[dim])
        up = [(i, (i + 1) % size) for i in range(size - 1)]
        down = [(j, i) for i, j in up]
        last = lax.slice_in_dim(shard, length - width, length, axis=dim)
        leading = lax.slice_in_dim(shard, 0, width, axis=dim)
        before = lax.ppermute(last, axis, up)
        after = lax.ppermute(leading, axis, down)
        shard = jnp.concatenate([before, shard, after], axis=dim)
    return shard


def cholesky_apply(factor, values):
    halfway = lax.linalg.triangular_solve(factor, values, left_side=True, lower=True)
    return lax.linalg.triangular_solve(
        factor, halfway, left_side=True, lower=True, transpose_a=True
    )


def take_columns(matrix, indices):
    return jnp.take(matrix, indices, axis=1)


def shards(acts, grads, picks):
    volumes, channels, planes, height, kernel_extent = acts.shape
    outputs = grads.shape[1]
    sample_count = picks.shape[1]
    plane_size = (height + 2) * (kernel_extent + 2)
    shifts = jnp.array(
        [
            along_z * plane_size + along_y * (kernel_extent + 2) + along_x
            for along_z in range(3)
            for along_y in range(3)
            for along_x in range(3)
        ],
        dtype=jnp.int32,
    )
    extended = padded_2(acts, (("slab", 2),), 1)
    padded = jnp.pad(extended, ((0, 0), (0, 0), (0, 0), (1, 1), (1, 1)))
    grad_rows = grads.reshape(volumes, outputs, -1)
    products = []
    for offset in range(27):
        along_z, along_y, along_x = (offset // 9, offset // 3 % 3, offset % 3)
        shifted = padded[
            :,
            :,
            along_z : along_z + planes,
            along_y : along_y + height,
            along_x : along_x + kernel_extent,
        ].reshape(volumes, channels, -1)
        products.append(
            lax.dot_general(
                grad_rows, shifted, (((0, 2), (0, 2)), ((), ())), preferred_element_type=jnp.float32
            )
        )
    gradient_portion = jnp.concatenate(products, axis=1)
    sample_index = jnp.arange(sample_count, dtype=jnp.int32)
    position = sample_index[None, :] * 32 + picks
    plane_index = position // (height * kernel_extent)
    row_index = position // kernel_extent % height
    column_index = position % kernel_extent
    base_index = plane_index * plane_size + row_index * (kernel_extent + 2) + column_index
    flat_index = (shifts[None, :, None] + base_index[:, None, :]).reshape(volumes, -1)
    selected_values = jax.vmap(take_columns)(padded.reshape(volumes, channels, -1), flat_index)
    input_patches = selected_values.reshape(volumes, channels, 27, sample_count).transpose(
        0, 2, 1, 3
    )
    grad_samples = jax.vmap(take_columns)(grad_rows, position)
    gradient_gram_matrix = jnp.einsum(
        "vcs,vds->cd", grad_samples, grad_samples, preferred_element_type=jnp.float32
    )
    gram = jnp.einsum(
        "mfuh,mioh->fuio", input_patches, input_patches, preferred_element_type=jnp.float32
    ).reshape(27 * channels, 27 * channels)
    summed_acts, summed_grads, summed_weight = lax.psum(
        (gram, gradient_gram_matrix, gradient_portion), ("dp", "slab")
    )
    positions = (
        volumes * lax.axis_size("dp") * planes * lax.axis_size("slab") * height * kernel_extent
    )
    samples = volumes * lax.axis_size("dp") * sample_count * lax.axis_size("slab")
    weight_grad = summed_weight / math.sqrt(positions)
    factor_acts = summed_acts / samples
    factor_grads = summed_grads / samples
    patch_width = factor_acts.shape[0]
    trace_ratio = jnp.sqrt(
        (jnp.trace(factor_acts) / patch_width + epsilon)
        / (jnp.trace(factor_grads) / outputs + epsilon)
    )
    damped_activation_factor = factor_acts + trace_ratio * math.sqrt(damping) * jnp.eye(
        patch_width, dtype=jnp.float32
    )
    damped_grads = factor_grads + math.sqrt(damping) / trace_ratio * jnp.eye(
        outputs, dtype=jnp.float32
    )
    chol_acts = jnp.linalg.cholesky(damped_activation_factor)
    chol_grads = jnp.linalg.cholesky(damped_grads)
    left_solved = cholesky_apply(chol_grads, weight_grad)
    precond = cholesky_apply(chol_acts, left_solved.T).T
    quadratic = jnp.sum(precond * weight_grad)
    clip_factor = jnp.minimum(1.0, jnp.sqrt(trust_region_limit / (learning_rate**2 * quadratic)))
    return (weight_grad, clip_factor * precond)


def solution(mesh):
    return jax.shard_map(
        shards,
        mesh=mesh,
        in_specs=(
            P("dp", None, "slab", None, None),
            P("dp", None, "slab", None, None),
            P("dp", "slab"),
        ),
        out_specs=(P(), P()),
        check_vma=False,
    )
```

profile of v0, /device:TPU:0, one launch (start us, length us, event | category | flops | bytes accessed | tf_op | source)
XLA Modules:
  0.0 786.8 jit_solution(2452920314638502882)
XLA Ops:
  9.1 4.9 collective-permute-start
  18.2 2.8 convolution_bitcast_fusion.13
  21.0 37.8 %collective-permute-done = bf16[1,32,1,128,128]{4,1,3,2,0:T(8,128)(2,1)S(1)} collective-permute-done((bf16[1,32,1,128,128]{4,1,3,2,0:T(8,128)(2,1)S(1)}, bf16[1,32,1,128,128]{4,1,3,2,0:T(8,128)(2,1)S(1)}, u32[]{:S(2)}, u32[]{:S(2)}) %collective-permute-start) | collective-permute-done | bytes 1048608 | tf_op jit(solution)/shard_map/ppermute | solution.py:20
  58.9 7.8 select_maximum_fusion
  93.4 6.5 copy.71
  99.9 6.9 reshape.605
  106.8 8.9 %copy.72 = bf16[1,32,50700]{1,2,0:T(8,128)(2,1)} copy(bf16[1,32,50700]{2,1,0:T(8,128)(2,1)S(1)} %reshape.605) | data formatting | bytes 6489600 | tf_op jit(solution)/shard_map/reshape | solution.py:77
  115.7 209.4 %gather_fusion = bf16[13824,32]{1,0:T(8,128)(2,1)} fusion(bf16[1,32,50700]{1,2,0:T(8,128)(2,1)} %copy.72, s32[13824]{0:T(1024)S(1)} %fusion.81), kind=kCustom, calls=%fused_computation | custom fusion | bytes 1880064 | tf_op jit(solution)/shard_map/vmap(jit(_take))/gather | solution.py:34
  325.2 3.2 copy.73
  328.6 2.8 fusion.151
  334.0 3.3 copy.74
  337.4 6.0 gather_fusion.1
  343.8 41.9 %psum.23 = f32[32,32]{1,0:T(8,128)S(1)} all-reduce(f32[32,32]{1,0:T(8,128)S(1)} %fusion.34), channel_id=1, replica_groups=mesh['dp'=4,'slab'=8] {'dp','slab'}, use_global_device_ids=true, to_apply=%region_3.4 | all-reduce | flops 1024 | bytes 8192 | tf_op jit(solution)/shard_map/psum | solution.py:88
  387.6 88.0 %all-reduce.7.cloned.1.call-done = (f32[32,864]{1,0:T(8,128)}, f32[864,864]{1,0:T(8,128)}) async-done(((f32[32,864]{1,0:T(8,128)}, f32[864,864]{1,0:T(8,128)}), (f32[32,864]{1,0:T(8,128)}, f32[864,864]{1,0:T(8,128)})) %all-reduce.7.cloned.1.call-update) | async-done | bytes 3096592 | tf_op jit(solution)/shard_map/psum | solution.py:88
  481.0 4.7 copy.75
  489.6 11.7 %cholesky.204 = f32[128,128]{1,0:T(8,128)S(1)} custom-call(f32[128,128]{1,0:T(8,128)S(1)} %cholesky.534), custom_call_target="Cholesky" | custom-call | tf_op jit(solution)/shard_map/jit(cholesky)/cholesky | solution.py:109
  501.6 9.8 %custom-call.64 = f32[1,128,128]{1,2,0:T(8,128)S(1)} custom-call(f32[1,128,128]{2,1,0:T(8,128)S(1)} %get-tuple-element.40), custom_call_target="InvertDiagBlocksLowerTriangular" | custom-call | tf_op jit(solution)/shard_map/jit(cholesky)/cholesky | solution.py:109
  514.9 13.2 %cholesky.227 = f32[128,128]{1,0:T(8,128)} custom-call(f32[128,128]{1,0:T(8,128)} %cholesky.538), custom_call_target="Cholesky" | custom-call | tf_op jit(solution)/shard_map/jit(cholesky)/cholesky | solution.py:109
  529.6 11.4 %custom-call.65 = f32[1,128,128]{1,2,0:T(8,128)} custom-call(f32[1,128,128]{2,1,0:T(8,128)} %get-tuple-element.37), custom_call_target="InvertDiagBlocksLowerTriangular" | custom-call | tf_op jit(solution)/shard_map/jit(cholesky)/cholesky | solution.py:109
  543.9 12.3 %cholesky.432 = f32[128,128]{1,0:T(8,128)} custom-call(f32[128,128]{1,0:T(8,128)S(1)} %cholesky.543), custom_call_target="Cholesky" | custom-call | tf_op jit(solution)/shard_map/jit(cholesky)/cholesky | solution.py:109
  557.8 10.4 %custom-call.66 = f32[1,128,128]{1,2,0:T(8,128)} custom-call(f32[1,128,128]{2,1,0:T(8,128)S(1)} %get-tuple-element.34), custom_call_target="InvertDiagBlocksLowerTriangular" | custom-call | tf_op jit(solution)/shard_map/jit(cholesky)/cholesky | solution.py:109
  571.1 11.9 %cholesky.451 = f32[128,128]{1,0:T(8,128)S(1)} custom-call(f32[128,128]{1,0:T(8,128)S(1)} %cholesky.548), custom_call_target="Cholesky" | custom-call | tf_op jit(solution)/shard_map/jit(cholesky)/cholesky | solution.py:109
  583.8 9.8 %custom-call.67 = f32[1,128,128]{1,2,0:T(8,128)S(1)} custom-call(f32[1,128,128]{2,1,0:T(8,128)S(1)} %get-tuple-element.31), custom_call_target="InvertDiagBlocksLowerTriangular" | custom-call | tf_op jit(solution)/shard_map/jit(cholesky)/cholesky | solution.py:109
  595.6 11.7 %cholesky.470 = f32[128,128]{1,0:T(8,128)S(1)} custom-call(f32[128,128]{1,0:T(8,128)S(1)} %cholesky.553), custom_call_target="Cholesky" | custom-call | tf_op jit(solution)/shard_map/jit(cholesky)/cholesky | solution.py:109
  608.0 9.8 %custom-call.68 = f32[1,128,128]{1,2,0:T(8,128)S(1)} custom-call(f32[1,128,128]{2,1,0:T(8,128)S(1)} %get-tuple-element.28), custom_call_target="InvertDiagBlocksLowerTriangular" | custom-call | tf_op jit(solution)/shard_map/jit(cholesky)/cholesky | solution.py:109
  619.7 12.1 %cholesky.490 = f32[128,128]{1,0:T(8,128)S(1)} custom-call(f32[128,128]{1,0:T(8,128)S(1)} %cholesky.558), custom_call_target="Cholesky" | custom-call | tf_op jit(solution)/shard_map/jit(cholesky)/cholesky | solution.py:109
  632.4 9.8 %custom-call.69 = f32[1,128,128]{1,2,0:T(8,128)S(1)} custom-call(f32[1,128,128]{2,1,0:T(8,128)S(1)} %get-tuple-element.25), custom_call_target="InvertDiagBlocksLowerTriangular" | custom-call | tf_op jit(solution)/shard_map/jit(cholesky)/cholesky | solution.py:109
  643.6 8.8 %cholesky.511 = f32[96,96]{1,0:T(8,128)S(1)} custom-call(f32[96,96]{1,0:T(8,128)S(1)} %convolution_subtract_fusion.5), custom_call_target="Cholesky" | custom-call | tf_op jit(solution)/shard_map/jit(cholesky)/cholesky | solution.py:109
  660.3 18.0 %while.1 = (s32[]{:T(128)}, f32[864,864]{1,0:T(8,128)}, s32[6,2]{0,1:T(2,128)S(1)}, f32[6,128,128]{2,1,0:T(8,128)S(1)}, s32[]{:T(128)}) while((s32[]{:T(128)}, f32[864,864]{1,0:T(8,128)}, s32[6,2]{0,1:T(2,128)S(1)}, f32[6,128,128]{2,1,0:T(8,128)S(1)}, s32[]{:T(128)}) %tuple.58), condition=%wide.while_cond, body=%wide.while_body.sunk | while | flops 2 | bytes 131181 | solution.py:28
  680.2 69.7 %custom-call.70 = f32[7,128,128]{1,2,0:T(8,128)S(1)} custom-call(f32[7,128,128]{2,1,0:T(8,128)} %pad_maximum_fusion), custom_call_target="InvertDiagBlocksLowerTriangular" | custom-call | tf_op jit(solution)/shard_map/triangular_solve | solution.py:28
  754.0 4.2 cholesky.524
  761.6 3.8 custom-call.71
  (215 shorter events, 109.1 us)
Async XLA Ops:
  7.2 468.4 %all-reduce.7.cloned.1.call-start = ((), (), s32[]{:S(2)}) async-start(), calls=%async_computation | async-start | bytes 6422528 | tf_op jit(solution)/shard_map/psum | solution.py:88
  9.1 49.7 %collective-permute-start = (bf16[1,32,1,128,128]{4,1,3,2,0:T(8,128)(2,1)S(1)}, bf16[1,32,1,128,128]{4,1,3,2,0:T(8,128)(2,1)S(1)}, u32[]{:S(2)}, u32[]{:S(2)}) collective-permute-start(bf16[1,32,1,128,128]{4,1,3,2,0:T(8,128)(2,1)S(1)} %copy.40), channel_id=1, source_target_pairs={{0,1},{1,2},{2,3},{3,4},{4,5},{5,6},{6,7},{8,9},{9,10},{10,11},{11... | collective-permute-start | bytes 3145736 | tf_op jit(solution)/shard_map/ppermute | solution.py:20
  14.1 44.8 %collective-permute-start.1 = (bf16[1,32,1,128,128]{4,1,3,2,0:T(8,128)(2,1)S(1)}, bf16[1,32,1,128,128]{4,1,3,2,0:T(8,128)(2,1)S(1)}, u32[]{:S(2)}, u32[]{:S(2)}) collective-permute-start(bf16[1,32,1,128,128]{4,1,3,2,0:T(8,128)(2,1)S(1)} %copy.40), channel_id=1, source_target_pairs={{1,0},{2,1},{3,2},{4,3},{5,4},{6,5},{7,6},{9,8},{10,9},{11,10},{12... | collective-permute-start | bytes 3145736 | tf_op jit(solution)/shard_map/ppermute | solution.py:21
  21.0 45.7 %copy-start.4 = (bf16[1,32,1,128,128]{4,3,2,1,0:T(8,128)(2,1)S(1)}, bf16[1,32,1,128,128]{4,3,2,1,0:T(8,128)(2,1)}, u32[]{:S(2)}) copy-start(bf16[1,32,1,128,128]{4,3,2,1,0:T(8,128)(2,1)} %param.5) | copy-start | bytes 3145732
  58.9 7.8 copy-start.6
  58.9 7.8 copy-start.8
  328.4 2.9 copy-start.5
  328.4 2.9 copy-start.7
  328.6 3.7 copy-start.9
  331.3 1.8 copy-start.14
  331.3 1.8 copy-start.15
  331.4 1.8 copy-start.16
  331.4 1.8 copy-start.17
  331.4 1.8 copy-start.18
  331.4 1.8 copy-start.19
  331.4 1.8 copy-start.20
  331.4 1.8 copy-start.21
  331.4 1.8 copy-start.22
  331.4 1.8 copy-start.23
  331.4 1.8 copy-start.24
  334.0 3.4 copy-start.25
  385.7 1.9 copy-start.13
  475.6 3.5 copy-start
  487.9 1.6 copy-start.3
  658.4 0.9 copy-start.26
  658.4 1.9 copy-start.12
  658.6 1.7 copy-start.1
  678.3 94.2 %copy-start.2 = (f32[864,864]{1,0:T(8,128)S(1)}, f32[864,864]{1,0:T(8,128)}, u32[]{:S(2)}) copy-start(f32[864,864]{1,0:T(8,128)} %get-tuple-element.120) | copy-start | bytes 8957956
  766.3 11.4 %copy-start.11 = (f32[32,864]{1,0:T(8,128)}, f32[32,864]{1,0:T(8,128)S(1)}, u32[]{:S(2)}) copy-start(f32[32,864]{1,0:T(8,128)S(1)} %broadcast_multiply_fusion) | copy-start | bytes 331780
  766.3 11.4 %copy-start.10 = (f32[32,864]{1,0:T(8,128)S(1)}, f32[32,864]{1,0:T(8,128)}, u32[]{:S(2)}) copy-start(f32[32,864]{1,0:T(8,128)} %get-tuple-element.18) | copy-start | bytes 331780
Sparse Core Ops, SparseCore 0:
  334.2 141.3 all-reduce.6
where the time goes:
time: 794 us; the launch traced here: 787 us
  local copies, waits for them, and re-layouts  276 us (35%)
  other arithmetic  255 us (32%)
  waiting for transfers between devices  126 us (16%)
  matrix products  59 us (7%)
  blocking collectives  41.9 us (5%)
  between operations  22 us (3%)
    gather x5, local copies, waits for them, and re-layouts, take_columns(): return jnp.take(matrix, indices, axis=1)  219 us
    another operation x26, other arithmetic, shards(): chol_acts = jnp.linalg.cholesky(damped_activation_factor)  149 us
    psum x1, waiting for transfers between devices, shards(): lax.psum((gram, gradient_gram_matrix, gradient_portion), ('dp', 'slab'))  88 us
    another operation x9, other arithmetic, cholesky_apply(): lax.linalg.triangular_solve(factor, halfway, left_side=True, lower=True,...  78.2 us
    psum x1, blocking collectives, shards(): lax.psum((gram, gradient_gram_matrix, gradient_portion), ('dp', 'slab'))  41.9 us
    ppermute x1, waiting for transfers between devices, padded_2(): before = lax.ppermute(last, axis, up)  37.8 us
    dot_general x27, matrix products, shards(): lax.dot_general(grad_rows, shifted, (((0, 2), (0, 2)), ((), ())), preferr...  31.2 us
    another operation x18, local copies, waits for them, and re-layouts  17.9 us
  transfers between devices with their start and end apart: 3, of which 2 were waited for; matrix products, arithmetic and copies ran while one was open for 2% of the time, Pallas kernels for 0%

commit v1 on v0

--- a/solution.py
+++ b/solution.py
@@ -1,3 +1,4 @@
+import functools
 import math
 import jax
 import jax.numpy as jnp
@@ -8,6 +9,14 @@
 damping = 0.1
 trust_region_limit = 0.3
 learning_rate = 0.01
+
+
+def pipes_turn(a0, bus_axis, axis_name):
+    work_now = lax.psum(a0, bus_axis)
+    return lax.psum(work_now, axis_name)
+
+
+tiles_lay = functools.partial(pipes_turn, bus_axis="slab", axis_name="dp")
 
 
 def padded_2(shard, sides, width):
@@ -85,8 +94,8 @@
     gram = jnp.einsum(
         "mfuh,mioh->fuio", input_patches, input_patches, preferred_element_type=jnp.float32
     ).reshape(27 * channels, 27 * channels)
-    summed_acts, summed_grads, summed_weight = lax.psum(
-        (gram, gradient_gram_matrix, gradient_portion), ("dp", "slab")
+    summed_acts, summed_grads, summed_weight = tiles_lay(
+        (gram, gradient_gram_matrix, gradient_portion)
     )
     positions = (
         volumes * lax.axis_size("dp") * planes * lax.axis_size("slab") * height * kernel_extent

time: 794 us -> 856 us (1.078)
  waiting for transfers between devices: 126 us -> 184 us
    psum x1 -> x2, waiting for transfers between devices: 88 us -> 147 us  [the longest x1 134 us: pipes_turn(): work_now = lax.psum(a0, bus_axis)]
    psum x1 -> x2, blocking collectives: 41.9 us -> 46.6 us  [the longest x1 34.8 us: pipes_turn(): work_now = lax.psum(a0, bus_axis)]
  transfers between devices with their start and end apart: 3 -> 4, of which waited for: 2 -> 3; matrix products, arithmetic and copies ran while one was open for 2% -> 2% of each run, Pallas kernels for 0% -> 0%
where the time goes in v1:
time: 856 us; the launch traced here: 849 us
  local copies, waits for them, and re-layouts  276 us (32%)
  other arithmetic  255 us (30%)
  waiting for transfers between devices  184 us (21%)
  matrix products  59 us (7%)
  blocking collectives  46.6 us (5%)
  between operations  21.9 us (3%)
    gather x5, local copies, waits for them, and re-layouts, take_columns(): return jnp.take(matrix, indices, axis=1)  219 us
    another operation x26, other arithmetic, shards(): chol_acts = jnp.linalg.cholesky(damped_activation_factor)  149 us
    psum x1, waiting for transfers between devices, pipes_turn(): work_now = lax.psum(a0, bus_axis)  134 us
    another operation x9, other arithmetic, cholesky_apply(): lax.linalg.triangular_solve(factor, halfway, left_side=True, lower=True,...  78.2 us
    ppermute x1, waiting for transfers between devices, padded_2(): before = lax.ppermute(last, axis, up)  37.8 us
    psum x1, blocking collectives, pipes_turn(): work_now = lax.psum(a0, bus_axis)  34.8 us
    dot_general x27, matrix products, shards(): lax.dot_general(grad_rows, shifted, (((0, 2), (0, 2)), ((), ())), preferr...  31.2 us
    another operation x18, local copies, waits for them, and re-layouts  17.4 us
  transfers between devices with their start and end apart: 4, of which 3 were waited for; matrix products, arithmetic and copies ran while one was open for 2% of the time, Pallas kernels for 0%

profile of v1, /device:TPU:0, one launch (start us, length us, event | category | flops | bytes accessed | tf_op | source)
XLA Modules:
  0.0 849.3 jit_solution(3382944170378576890)
XLA Ops:
  9.1 4.9 collective-permute-start
  21.0 37.8 %collective-permute-done = bf16[1,32,1,128,128]{4,1,3,2,0:T(8,128)(2,1)S(1)} collective-permute-done((bf16[1,32,1,128,128]{4,1,3,2,0:T(8,128)(2,1)S(1)}, bf16[1,32,1,128,128]{4,1,3,2,0:T(8,128)(2,1)S(1)}, u32[]{:S(2)}, u32[]{:S(2)}) %collective-permute-start) | collective-permute-done | bytes 1048608 | tf_op jit(solution)/shard_map/ppermute | solution.py:29
  58.9 7.8 select_maximum_fusion
  93.4 6.5 copy.71
  99.9 6.9 reshape.605
  106.8 8.9 %copy.72 = bf16[1,32,50700]{1,2,0:T(8,128)(2,1)} copy(bf16[1,32,50700]{2,1,0:T(8,128)(2,1)S(1)} %reshape.605) | data formatting | bytes 6489600 | tf_op jit(solution)/shard_map/reshape | solution.py:86
  115.7 209.4 %gather_fusion = bf16[13824,32]{1,0:T(8,128)(2,1)} fusion(bf16[1,32,50700]{1,2,0:T(8,128)(2,1)} %copy.72, s32[13824]{0:T(1024)S(1)} %fusion.81), kind=kCustom, calls=%fused_computation | custom fusion | bytes 1880064 | tf_op jit(solution)/shard_map/vmap(jit(_take))/gather | solution.py:43
  325.2 3.2 copy.73
  334.1 133.5 %all-reduce.9.cloned.1.call-done = (f32[32,864]{1,0:T(8,128)}, f32[864,864]{1,0:T(8,128)}) async-done(((f32[32,864]{1,0:T(8,128)}, f32[864,864]{1,0:T(8,128)}), (f32[32,864]{1,0:T(8,128)}, f32[864,864]{1,0:T(8,128)})) %all-reduce.9.cloned.1.call-update) | async-done | bytes 3096592 | tf_op jit(solution)/shard_map/psum | solution.py:15
  467.6 3.3 copy.74
  471.0 6.1 gather_fusion.1
  477.5 34.8 %psum.46 = f32[32,32]{1,0:T(8,128)S(1)} all-reduce(f32[32,32]{1,0:T(8,128)S(1)} %fusion.34), channel_id=1, replica_groups=mesh['dp'=4,'slab'=8] {'slab'}, use_global_device_ids=true, to_apply=%region_5.6 | all-reduce | flops 1024 | bytes 8192 | tf_op jit(solution)/shard_map/psum | solution.py:15
  512.3 11.7 %psum.47 = f32[32,32]{1,0:T(8,128)S(1)} all-reduce(f32[32,32]{1,0:T(8,128)S(1)} %psum.46), channel_id=1, replica_groups=mesh['dp'=4,'slab'=8] {'dp'}, use_global_device_ids=true, to_apply=%region_6.7 | all-reduce | flops 1024 | bytes 8192 | tf_op jit(solution)/shard_map/psum | solution.py:16
  525.9 13.0 %all-reduce.11.cloned.1.call-done = (f32[32,864]{1,0:T(8,128)}, f32[864,864]{1,0:T(8,128)}) async-done(((f32[32,864]{1,0:T(8,128)}, f32[864,864]{1,0:T(8,128)}), (f32[32,864]{1,0:T(8,128)}, f32[864,864]{1,0:T(8,128)})) %all-reduce.11.cloned.1.call-update) | async-done | bytes 3096592 | tf_op jit(solution)/shard_map/psum | solution.py:16
  544.3 4.7 copy.75
  552.9 11.7 %cholesky.204 = f32[128,128]{1,0:T(8,128)S(1)} custom-call(f32[128,128]{1,0:T(8,128)S(1)} %cholesky.534), custom_call_target="Cholesky" | custom-call | tf_op jit(solution)/shard_map/jit(cholesky)/cholesky | solution.py:118
  564.9 9.8 %custom-call.64 = f32[1,128,128]{1,2,0:T(8,128)S(1)} custom-call(f32[1,128,128]{2,1,0:T(8,128)S(1)} %get-tuple-element.42), custom_call_target="InvertDiagBlocksLowerTriangular" | custom-call | tf_op jit(solution)/shard_map/jit(cholesky)/cholesky | solution.py:118
  578.2 13.2 %cholesky.227 = f32[128,128]{1,0:T(8,128)} custom-call(f32[128,128]{1,0:T(8,128)} %cholesky.538), custom_call_target="Cholesky" | custom-call | tf_op jit(solution)/shard_map/jit(cholesky)/cholesky | solution.py:118
  592.9 11.4 %custom-call.65 = f32[1,128,128]{1,2,0:T(8,128)} custom-call(f32[1,128,128]{2,1,0:T(8,128)} %get-tuple-element.39), custom_call_target="InvertDiagBlocksLowerTriangular" | custom-call | tf_op jit(solution)/shard_map/jit(cholesky)/cholesky | solution.py:118
  607.2 12.3 %cholesky.432 = f32[128,128]{1,0:T(8,128)} custom-call(f32[128,128]{1,0:T(8,128)S(1)} %cholesky.543), custom_call_target="Cholesky" | custom-call | tf_op jit(solution)/shard_map/jit(cholesky)/cholesky | solution.py:118
  621.0 10.4 %custom-call.66 = f32[1,128,128]{1,2,0:T(8,128)} custom-call(f32[1,128,128]{2,1,0:T(8,128)S(1)} %get-tuple-element.36), custom_call_target="InvertDiagBlocksLowerTriangular" | custom-call | tf_op jit(solution)/shard_map/jit(cholesky)/cholesky | solution.py:118
  634.4 11.9 %cholesky.451 = f32[128,128]{1,0:T(8,128)S(1)} custom-call(f32[128,128]{1,0:T(8,128)S(1)} %cholesky.548), custom_call_target="Cholesky" | custom-call | tf_op jit(solution)/shard_map/jit(cholesky)/cholesky | solution.py:118
  647.0 9.8 %custom-call.67 = f32[1,128,128]{1,2,0:T(8,128)S(1)} custom-call(f32[1,128,128]{2,1,0:T(8,128)S(1)} %get-tuple-element.33), custom_call_target="InvertDiagBlocksLowerTriangular" | custom-call | tf_op jit(solution)/shard_map/jit(cholesky)/cholesky | solution.py:118
  658.8 11.7 %cholesky.470 = f32[128,128]{1,0:T(8,128)S(1)} custom-call(f32[128,128]{1,0:T(8,128)S(1)} %cholesky.553), custom_call_target="Cholesky" | custom-call | tf_op jit(solution)/shard_map/jit(cholesky)/cholesky | solution.py:118
  671.3 9.8 %custom-call.68 = f32[1,128,128]{1,2,0:T(8,128)S(1)} custom-call(f32[1,128,128]{2,1,0:T(8,128)S(1)} %get-tuple-element.30), custom_call_target="InvertDiagBlocksLowerTriangular" | custom-call | tf_op jit(solution)/shard_map/jit(cholesky)/cholesky | solution.py:118
  682.9 12.1 %cholesky.490 = f32[128,128]{1,0:T(8,128)S(1)} custom-call(f32[128,128]{1,0:T(8,128)S(1)} %cholesky.558), custom_call_target="Cholesky" | custom-call | tf_op jit(solution)/shard_map/jit(cholesky)/cholesky | solution.py:118
  695.7 9.8 %custom-call.69 = f32[1,128,128]{1,2,0:T(8,128)S(1)} custom-call(f32[1,128,128]{2,1,0:T(8,128)S(1)} %get-tuple-element.27), custom_call_target="InvertDiagBlocksLowerTriangular" | custom-call | tf_op jit(solution)/shard_map/jit(cholesky)/cholesky | solution.py:118
  706.9 8.8 %cholesky.511 = f32[96,96]{1,0:T(8,128)S(1)} custom-call(f32[96,96]{1,0:T(8,128)S(1)} %convolution_subtract_fusion.5), custom_call_target="Cholesky" | custom-call | tf_op jit(solution)/shard_map/jit(cholesky)/cholesky | solution.py:118
  723.4 17.5 %while.1 = (s32[]{:T(128)}, f32[864,864]{1,0:T(8,128)}, s32[6,2]{0,1:T(2,128)S(1)}, f32[6,128,128]{2,1,0:T(8,128)S(1)}, s32[]{:T(128)}) while((s32[]{:T(128)}, f32[864,864]{1,0:T(8,128)}, s32[6,2]{0,1:T(2,128)S(1)}, f32[6,128,128]{2,1,0:T(8,128)S(1)}, s32[]{:T(128)}) %tuple.61), condition=%wide.while_cond, body=%wide.while_body.sunk | while | flops 2 | bytes 131181 | solution.py:37
  742.7 69.7 %custom-call.70 = f32[7,128,128]{1,2,0:T(8,128)S(1)} custom-call(f32[7,128,128]{2,1,0:T(8,128)} %pad_maximum_fusion), custom_call_target="InvertDiagBlocksLowerTriangular" | custom-call | tf_op jit(solution)/shard_map/triangular_solve | solution.py:37
  816.5 4.2 cholesky.524
  824.1 3.8 custom-call.71
  (219 shorter events, 114.1 us)
Async XLA Ops:
  7.2 460.4 %all-reduce.9.cloned.1.call-start = ((), (), s32[]{:S(2)}) async-start(), calls=%async_computation | async-start | bytes 6422528 | tf_op jit(solution)/shard_map/psum | solution.py:15
  9.1 49.7 %collective-permute-start = (bf16[1,32,1,128,128]{4,1,3,2,0:T(8,128)(2,1)S(1)}, bf16[1,32,1,128,128]{4,1,3,2,0:T(8,128)(2,1)S(1)}, u32[]{:S(2)}, u32[]{:S(2)}) collective-permute-start(bf16[1,32,1,128,128]{4,1,3,2,0:T(8,128)(2,1)S(1)} %copy.40), channel_id=1, source_target_pairs={{0,1},{1,2},{2,3},{3,4},{4,5},{5,6},{6,7},{8,9},{9,10},{10,11},{11... | collective-permute-start | bytes 3145736 | tf_op jit(solution)/shard_map/ppermute | solution.py:29
  14.1 44.8 %collective-permute-start.1 = (bf16[1,32,1,128,128]{4,1,3,2,0:T(8,128)(2,1)S(1)}, bf16[1,32,1,128,128]{4,1,3,2,0:T(8,128)(2,1)S(1)}, u32[]{:S(2)}, u32[]{:S(2)}) collective-permute-start(bf16[1,32,1,128,128]{4,1,3,2,0:T(8,128)(2,1)S(1)} %copy.40), channel_id=1, source_target_pairs={{1,0},{2,1},{3,2},{4,3},{5,4},{6,5},{7,6},{9,8},{10,9},{11,10},{12... | collective-permute-start | bytes 3145736 | tf_op jit(solution)/shard_map/ppermute | solution.py:30
  21.0 45.7 %copy-start.4 = (bf16[1,32,1,128,128]{4,3,2,1,0:T(8,128)(2,1)S(1)}, bf16[1,32,1,128,128]{4,3,2,1,0:T(8,128)(2,1)}, u32[]{:S(2)}) copy-start(bf16[1,32,1,128,128]{4,3,2,1,0:T(8,128)(2,1)} %param.5) | copy-start | bytes 3145732
  58.9 7.8 copy-start.6
  58.9 7.8 copy-start.8
  328.4 2.9 copy-start.5
  328.4 2.9 copy-start.7
  328.6 3.7 copy-start.9
  331.3 1.8 copy-start.14
  331.3 1.8 copy-start.15
  331.3 1.8 copy-start.16
  331.4 1.8 copy-start.17
  331.4 1.8 copy-start.18
  331.4 1.8 copy-start.19
  331.4 1.8 copy-start.20
  331.4 1.8 copy-start.21
  331.4 1.8 copy-start.22
  331.4 1.8 copy-start.23
  331.4 1.8 copy-start.24
  334.0 204.9 %all-reduce.11.cloned.1.call-start = ((), (), s32[]{:S(2)}) async-start(), calls=%async_computation.1 | async-start | bytes 6422528 | tf_op jit(solution)/shard_map/psum | solution.py:16
  467.6 3.4 copy-start.25
  524.0 1.9 copy-start.13
  538.9 3.5 copy-start
  551.2 1.6 copy-start.3
  721.4 0.9 copy-start.26
  721.4 1.9 copy-start.12
  721.7 1.7 copy-start.1
  740.8 94.2 %copy-start.2 = (f32[864,864]{1,0:T(8,128)S(1)}, f32[864,864]{1,0:T(8,128)}, u32[]{:S(2)}) copy-start(f32[864,864]{1,0:T(8,128)} %get-tuple-element.126) | copy-start | bytes 8957956
  828.8 11.4 %copy-start.11 = (f32[32,864]{1,0:T(8,128)}, f32[32,864]{1,0:T(8,128)S(1)}, u32[]{:S(2)}) copy-start(f32[32,864]{1,0:T(8,128)S(1)} %broadcast_multiply_fusion) | copy-start | bytes 331780
  828.8 11.4 %copy-start.10 = (f32[32,864]{1,0:T(8,128)S(1)}, f32[32,864]{1,0:T(8,128)}, u32[]{:S(2)}) copy-start(f32[32,864]{1,0:T(8,128)} %get-tuple-element.20) | copy-start | bytes 331780
Sparse Core Ops, SparseCore 0:
  334.1 133.4 all-reduce.8
  470.0 68.8 all-reduce.10
